TPU v7x, 32 devices: a whole 2x2x4 slice. The times are simulated.
32 devices in a mesh: dp: 8 (over y, x, core), tensor: 4 (over z).
Axes of the slice: x: 2, y: 2, z: 4, core: 2. Of those that a mesh axis runs over, the one named last changes fastest.
Arguments:
- tokens: bfloat16 [32, 256, 1152], P(('dp', 'tensor')), may hold values from -6 to 6
- timesteps: int32 [32], P('dp'), may hold values from 0 to 999
- labels: int32 [32], P('dp'), may hold values from 0 to 999
- item_counts: int32 [8], P('dp'), may hold values from 1 to 4
- cotangent: bfloat16 [32, 256, 1152], P(('dp', 'tensor')), may hold values from -6 to 6
- project_weight: bfloat16 [1152, 3, 1152], P(None, None, 'tensor'), may hold values from -0.1875 to 0.1875
- query_gain: bfloat16 [72], replicated, may hold values from 0.099609375 to 1.8984375
- key_gain: bfloat16 [72], replicated, may hold values from 0.099609375 to 1.8984375
- output_weight: bfloat16 [1152, 1152], P('tensor'), may hold values from -0.5 to 0.5
- output_bias: bfloat16 [1152], replicated, may hold values from -3 to 3
- expand_weight: bfloat16 [1152, 2, 3072], P(None, None, 'tensor'), may hold values from -0.1875 to 0.1875
- down_weight: bfloat16 [3072, 1152], P('tensor'), may hold values from -0.15625 to 0.15625
- down_bias: bfloat16 [1152], replicated, may hold values from -3 to 3
- modulate_weight: bfloat16 [1152, 6, 1152], P(None, None, 'tensor'), may hold values from -0.1875 to 0.1875
- modulate_bias: bfloat16 [6, 1152], P(None, 'tensor'), may hold values from -3 to 3
- time_weight: bfloat16 [256, 1152], replicated, may hold values from -0.5 to 0.5
- time_bias: bfloat16 [1152], replicated, may hold values from -3 to 3
- embed_weight: bfloat16 [1152, 1152], replicated, may hold values from -0.25 to 0.25
- embed_bias: bfloat16 [1152], replicated, may hold values from -3 to 3
- class_table: bfloat16 [1000, 1152], replicated, may hold values from -6 to 6
Outputs:
- result: bfloat16 [32, 256, 1152], P(('dp', 'tensor'))
- tokens_grad: bfloat16 [32, 256, 1152], P(('dp', 'tensor'))
- project_grad: float32 [1152, 3, 1152], P('dp', None, 'tensor')
- query_gain_grad: float32 [72], replicated
- key_gain_grad: float32 [72], replicated
- output_weight_grad: float32 [1152, 1152], P('tensor', 'dp')
- output_bias_grad: float32 [1152], replicated
- expand_grad: float32 [1152, 2, 3072], P('dp', None, 'tensor')
- down_grad: float32 [3072, 1152], P('tensor', 'dp')
- down_bias_grad: float32 [1152], replicated
- modulate_grad: float32 [1152, 6, 1152], P('dp', None, 'tensor')
- modulate_bias_grad: float32 [6, 1152], replicated
- time_grad: float32 [256, 1152], P(None, 'dp')
- time_bias_grad: float32 [1152], P('dp')
- embed_grad: float32 [1152, 1152], P('dp')
- embed_bias_grad: float32 [1152], P('dp')
- class_grad: float32 [1000, 1152], P(None, 'dp')
Inputs may be any that keep to these rules, and one draw needn't show every extreme that they name: `item_counts`: entry i counts the real items among the 4 items of index i of dp; they are its first ones.
All inputs are finite; a program needn't handle non-finite values.
Results may differ from a plain program's by a relative error of at most 0.03.
Values may be sent and summed in bfloat16 or wider, within the bound.
A program may use at most 256 MiB of HBM per device.

v0:
```python
import math
import jax
import jax.numpy as jnp
from jax import lax
from jax.sharding import PartitionSpec as P

HD = 72
FREQ = 256
GRID = 16
EPS = 1e-06


def layer_norm(value):
    center = value - jnp.mean(value, axis=-1, keepdims=True)
    inverse = lax.rsqrt(jnp.mean(center * center, axis=-1, keepdims=True) + EPS)
    return (center * inverse, inverse)


def layer_norm_back(normed, inverse, grad):
    return inverse * (
        grad
        - jnp.mean(grad, axis=-1, keepdims=True)
        - normed * jnp.mean(grad * normed, axis=-1, keepdims=True)
    )


def silu_slope(value):
    sigma = jax.nn.sigmoid(value)
    return sigma * (1.0 + value * (1.0 - sigma))


def rotate(value, positions):
    quarter = HD // 4
    rates = 10000.0 ** (-jnp.arange(quarter, dtype=jnp.float32) / quarter)
    places = ((positions // GRID).astype(jnp.float32), (positions % GRID).astype(jnp.float32))
    pieces = []
    for which_half in range(2):
        half_value = value[..., which_half * 2 * quarter : (which_half + 1) * 2 * quarter]
        angle = places[which_half][:, None] * rates[None, :]
        cosine = jnp.cos(angle)[None, :, None, :]
        sine = jnp.sin(angle)[None, :, None, :]
        first = half_value[..., :quarter]
        second = half_value[..., quarter:]
        pieces.append(first * cosine - second * sine)
        pieces.append(second * cosine + first * sine)
    return jnp.concatenate(pieces, axis=-1)


def head_prepare(raw, gain, positions):
    scaled = raw * lax.rsqrt(jnp.mean(raw * raw, axis=-1, keepdims=True) + EPS) * gain
    return rotate(scaled, positions)


def time_features(steps_in):
    half = FREQ // 2
    rates = jnp.exp(-math.log(10000.0) * jnp.arange(half, dtype=jnp.float32) / half)
    angle = steps_in.astype(jnp.float32)[:, None] * rates[None, :]
    return jnp.concatenate([jnp.cos(angle), jnp.sin(angle)], axis=-1)


def shards(
    tokens,
    timesteps,
    labels,
    item_counts,
    cotangent,
    project_weight,
    query_gain,
    key_gain,
    output_weight,
    output_bias,
    expand_weight,
    down_weight,
    down_bias,
    modulate_weight,
    modulate_bias,
    time_weight,
    time_bias,
    embed_weight,
    embed_bias,
    class_table,
):
    local_items, length, width = tokens.shape
    items = timesteps.shape[0]
    slab = modulate_weight.shape[2]
    heads_here = project_weight.shape[2] // HD
    scale = HD ** (-0.5)
    lane = lax.axis_index("tensor")
    first_item = lane * local_items
    live = (first_item + jnp.arange(local_items) < item_counts[0]).astype(jnp.float32)[
        :, None, None
    ]
    time_feat = time_features(timesteps).astype(jnp.bfloat16)
    pre_hidden = jnp.dot(
        time_feat, time_weight, preferred_element_type=jnp.float32
    ) + time_bias.astype(jnp.float32)
    time_hidden = jax.nn.silu(pre_hidden).astype(jnp.bfloat16)
    condition = (
        jnp.dot(time_hidden, embed_weight, preferred_element_type=jnp.float32)
        + embed_bias.astype(jnp.float32)
        + jnp.take(class_table, labels, axis=0).astype(jnp.float32)
    )
    cond_act = jax.nn.silu(condition).astype(jnp.bfloat16)
    modulation_part = (
        jnp.einsum("bd,dke->bke", cond_act, modulate_weight, preferred_element_type=jnp.float32)
        + modulate_bias.astype(jnp.float32)
    ).astype(jnp.bfloat16)
    token_all, modulation = (
        lax.all_gather(tokens, "tensor", axis=0, tiled=True),
        lax.all_gather(modulation_part, "tensor", axis=2, tiled=True),
    )
    modulation = modulation.astype(jnp.float32)
    modulation_local = lax.dynamic_slice_in_dim(modulation, first_item, local_items, 0)
    attend_shift_all = modulation[:, 0][:, None, :]
    attend_scale_all = modulation[:, 1][:, None, :]
    local_parts = [modulation_local[:, which][:, None, :] for which in range(6)]
    _, attend_scale, attend_gate, feed_shift, feed_scale, feed_gate = local_parts
    positions = jnp.arange(length)
    normed_all, _ = layer_norm(token_all.astype(jnp.float32))
    mod_in = (normed_all * (1.0 + attend_scale_all) + attend_shift_all).astype(jnp.bfloat16)
    projected = jnp.einsum(
        "bld,dke->blke", mod_in, project_weight, preferred_element_type=jnp.float32
    )
    split = projected.reshape(items, length, 3, heads_here, HD)
    query_gain_f = query_gain.astype(jnp.float32)
    key_gain_f = key_gain.astype(jnp.float32)
    queries = head_prepare(split[:, :, 0], query_gain_f, positions).astype(jnp.bfloat16)
    keys = head_prepare(split[:, :, 1], key_gain_f, positions).astype(jnp.bfloat16)
    values = split[:, :, 2].astype(jnp.bfloat16)
    scores = (
        jnp.einsum("bqhd,bkhd->bhqk", queries, keys, preferred_element_type=jnp.float32) * scale
    )
    top = jnp.max(scores, axis=-1, keepdims=True)
    logsum = top + jnp.log(jnp.sum(jnp.exp(scores - top), axis=-1, keepdims=True))
    probs = jnp.exp(scores - logsum).astype(jnp.bfloat16)
    mixed = jnp.einsum("bhqk,bkhd->bqhd", probs, values, preferred_element_type=jnp.float32)
    mixed = mixed.reshape(items, length, heads_here * HD).astype(jnp.bfloat16)
    piece = mixed
    attend_branch = lax.psum_scatter(
        jnp.einsum("blh,hd->bld", piece, output_weight, preferred_element_type=jnp.float32).astype(
            jnp.bfloat16
        ),
        "tensor",
        scatter_dimension=0,
        tiled=True,
    ).astype(jnp.float32) + output_bias.astype(jnp.float32)
    token_local = tokens.astype(jnp.float32)
    normed_local, inverse_local = layer_norm(token_local)
    residual = token_local + attend_gate * attend_branch
    normed_two, inverse_two = layer_norm(residual)
    mod_two = (normed_two * (1.0 + feed_scale) + feed_shift).astype(jnp.bfloat16)
    mod_two_all = lax.all_gather(mod_two, "tensor", axis=0, tiled=True)
    gate_up = jnp.einsum(
        "bld,dkf->blkf", mod_two_all, expand_weight, preferred_element_type=jnp.float32
    )
    gate = gate_up[:, :, 0]
    upper = gate_up[:, :, 1]
    hidden = (jax.nn.silu(gate) * upper).astype(jnp.bfloat16)
    piece = hidden
    feed_branch = lax.psum_scatter(
        jnp.einsum("blf,fd->bld", piece, down_weight, preferred_element_type=jnp.float32).astype(
            jnp.bfloat16
        ),
        "tensor",
        scatter_dimension=0,
        tiled=True,
    ).astype(jnp.float32) + down_bias.astype(jnp.float32)
    result = (live * (residual + feed_gate * feed_branch)).astype(jnp.bfloat16)
    out_grad = cotangent.astype(jnp.float32) * live
    branch_grad = (out_grad * feed_gate).astype(jnp.bfloat16)
    down_bias_part = jnp.sum(branch_grad.astype(jnp.float32), axis=(0, 1))
    piece = lax.all_gather(branch_grad, "tensor", axis=0, tiled=True)
    weight_total = jnp.einsum("blf,bld->fd", hidden, piece, preferred_element_type=jnp.float32)
    rows_grad = jnp.einsum("bld,fd->blf", piece, down_weight, preferred_element_type=jnp.float32)
    hidden_total = rows_grad
    down_grad = weight_total
    gate_up_grad = jnp.stack(
        [hidden_total * upper * silu_slope(gate), hidden_total * jax.nn.silu(gate)], axis=2
    ).astype(jnp.bfloat16)
    expand_grad = jnp.einsum(
        "bld,blkf->dkf", mod_two_all, gate_up_grad, preferred_element_type=jnp.float32
    )
    piece = gate_up_grad
    mod_two_grad = lax.psum_scatter(
        jnp.einsum(
            "blkf,dkf->bld", piece, expand_weight, preferred_element_type=jnp.float32
        ).astype(jnp.bfloat16),
        "tensor",
        scatter_dimension=0,
        tiled=True,
    ).astype(jnp.float32)
    residual_grad = out_grad + layer_norm_back(
        normed_two, inverse_two, mod_two_grad * (1.0 + feed_scale)
    )
    attend_grad = (residual_grad * attend_gate).astype(jnp.bfloat16)
    output_bias_part = jnp.sum(attend_grad.astype(jnp.float32), axis=(0, 1))
    piece = lax.all_gather(attend_grad, "tensor", axis=0, tiled=True)
    weight_total = jnp.einsum("blh,bld->hd", mixed, piece, preferred_element_type=jnp.float32)
    rows_grad = jnp.einsum("bld,hd->blh", piece, output_weight, preferred_element_type=jnp.float32)
    output_weight_grad = weight_total
    mixed_grad = rows_grad
    mixed_grad = mixed_grad.reshape(items, length, heads_here, HD).astype(jnp.bfloat16)
    again = jnp.einsum("bqhd,bkhd->bhqk", queries, keys, preferred_element_type=jnp.float32) * scale
    prob_float = jnp.exp(again - logsum)
    prob_low = prob_float.astype(jnp.bfloat16)
    prob_grad = jnp.einsum(
        "bqhd,bkhd->bhqk", mixed_grad, values, preferred_element_type=jnp.float32
    )
    score_grad = (
        prob_float * (prob_grad - jnp.sum(prob_float * prob_grad, axis=-1, keepdims=True))
    ).astype(jnp.bfloat16)
    query_grad = (
        jnp.einsum("bhqk,bkhd->bqhd", score_grad, keys, preferred_element_type=jnp.float32) * scale
    )
    key_grad = (
        jnp.einsum("bhqk,bqhd->bkhd", score_grad, queries, preferred_element_type=jnp.float32)
        * scale
    )
    value_grad = jnp.einsum(
        "bhqk,bqhd->bkhd", prob_low, mixed_grad, preferred_element_type=jnp.float32
    )

    def prepare_here(raw, gain):
        return head_prepare(raw, gain, positions)

    _, query_back = jax.vjp(prepare_here, split[:, :, 0], query_gain_f)
    raw_query_grad, query_gain_part = query_back(query_grad)
    _, key_back = jax.vjp(prepare_here, split[:, :, 1], key_gain_f)
    raw_key_grad, key_gain_part = key_back(key_grad)
    projected_grad = jnp.stack([raw_query_grad, raw_key_grad, value_grad], axis=2)
    projected_grad = projected_grad.reshape(items, length, 3, heads_here * HD).astype(jnp.bfloat16)
    project_grad = jnp.einsum(
        "bld,blke->dke", mod_in, projected_grad, preferred_element_type=jnp.float32
    )
    piece = projected_grad
    mod_in_grad = lax.psum_scatter(
        jnp.einsum(
            "blke,dke->bld", piece, project_weight, preferred_element_type=jnp.float32
        ).astype(jnp.bfloat16),
        "tensor",
        scatter_dimension=0,
        tiled=True,
    ).astype(jnp.float32)
    tokens_grad = (
        residual_grad
        + layer_norm_back(normed_local, inverse_local, mod_in_grad * (1.0 + attend_scale))
    ).astype(jnp.bfloat16)
    modulation_grad_part = jnp.stack(
        [
            jnp.sum(mod_in_grad, axis=1),
            jnp.sum(mod_in_grad * normed_local, axis=1),
            jnp.sum(residual_grad * attend_branch, axis=1),
            jnp.sum(mod_two_grad, axis=1),
            jnp.sum(mod_two_grad * normed_two, axis=1),
            jnp.sum(out_grad * feed_branch, axis=1),
        ],
        axis=1,
    )
    modulation_grad = lax.all_to_all(
        modulation_grad_part, "tensor", split_axis=2, concat_axis=0, tiled=True
    ).astype(jnp.bfloat16)
    modulate_bias_part = jnp.sum(modulation_grad.astype(jnp.float32), axis=0)
    cond_part = jnp.einsum(
        "bke,dke->bd", modulation_grad, modulate_weight, preferred_element_type=jnp.float32
    )
    cond_total = lax.psum(cond_part, "tensor")
    cond_grad = (cond_total * silu_slope(condition)).astype(jnp.bfloat16)
    one_hot = (labels[:, None] == jnp.arange(class_table.shape[0])[None, :]).astype(jnp.bfloat16)
    class_grad = jnp.einsum("bc,bd->cd", one_hot, cond_grad, preferred_element_type=jnp.float32)
    pre_grad = (
        jnp.einsum("be,de->bd", cond_grad, embed_weight, preferred_element_type=jnp.float32)
        * silu_slope(pre_hidden)
    ).astype(jnp.bfloat16)
    bias_wide = lax.dynamic_update_slice_in_dim(
        jnp.zeros((6, width), jnp.float32), modulate_bias_part, lane * slab, 1
    )
    output_bias_grad, down_bias_grad, query_gain_grad, key_gain_grad, modulate_bias_grad = lax.psum(
        (output_bias_part, down_bias_part, query_gain_part, key_gain_part, bias_wide),
        ("dp", "tensor"),
    )
    modulate_local = jnp.einsum(
        "bd,bke->dke", cond_act, modulation_grad, preferred_element_type=jnp.float32
    )
    embed_local = jnp.einsum(
        "bd,be->de", time_hidden, cond_grad, preferred_element_type=jnp.float32
    )
    embed_bias_local = jnp.sum(cond_grad.astype(jnp.float32), axis=0)
    time_local = jnp.einsum("bf,bd->fd", time_feat, pre_grad, preferred_element_type=jnp.float32)
    time_bias_local = jnp.sum(pre_grad.astype(jnp.float32), axis=0)
    (
        project_grad,
        output_weight_grad,
        expand_grad,
        down_grad,
        class_grad,
        modulate_grad,
        time_grad,
        time_bias_grad,
        embed_grad,
        embed_bias_grad,
    ) = (
        lax.psum_scatter(project_grad, "dp", scatter_dimension=0, tiled=True),
        lax.psum_scatter(output_weight_grad, "dp", scatter_dimension=1, tiled=True),
        lax.psum_scatter(expand_grad, "dp", scatter_dimension=0, tiled=True),
        lax.psum_scatter(down_grad, "dp", scatter_dimension=1, tiled=True),
        lax.psum_scatter(class_grad, "dp", scatter_dimension=1, tiled=True),
        lax.psum_scatter(modulate_local, "dp", scatter_dimension=0, tiled=True),
        lax.psum_scatter(time_local, "dp", scatter_dimension=1, tiled=True),
        lax.psum_scatter(time_bias_local, "dp", scatter_dimension=0, tiled=True),
        lax.psum_scatter(embed_local, "dp", scatter_dimension=0, tiled=True),
        lax.psum_scatter(embed_bias_local, "dp", scatter_dimension=0, tiled=True),
    )
    return (
        result,
        tokens_grad,
        project_grad,
        query_gain_grad,
        key_gain_grad,
        output_weight_grad,
        output_bias_grad,
        expand_grad,
        down_grad,
        down_bias_grad,
        modulate_grad,
        modulate_bias_grad,
        time_grad,
        time_bias_grad,
        embed_grad,
        embed_bias_grad,
        class_grad,
    )


def solution(mesh):
    return jax.shard_map(
        shards,
        mesh=mesh,
        in_specs=(
            P(("dp", "tensor"), None, None),
            P("dp"),
            P("dp"),
            P("dp"),
            P(("dp", "tensor"), None, None),
            P(None, None, "tensor"),
            P(),
            P(),
            P("tensor", None),
            P(),
            P(None, None, "tensor"),
            P("tensor", None),
            P(),
            P(None, None, "tensor"),
            P(None, "tensor"),
            P(),
            P(),
            P(),
            P(),
            P(),
        ),
        out_specs=(
            P(("dp", "tensor"), None, None),
            P(("dp", "tensor"), None, None),
            P("dp", None, "tensor"),
            P(),
            P(),
            P("tensor", "dp"),
            P(),
            P("dp", None, "tensor"),
            P("tensor", "dp"),
            P(),
            P("dp", None, "tensor"),
            P(),
            P(None, "dp"),
            P("dp"),
            P("dp", None),
            P("dp"),
            P(None, "dp"),
        ),
        check_vma=False,
    )
```

profile of v0, /device:TPU:0, one launch (start us, length us, event | category | flops | bytes accessed | tf_op | source)
XLA Modules:
  0.0 962.4 jit_solution(16076023338928004156)
XLA Ops:
  12.7 2.5 gather_fusion
  16.6 1.3 convolution_add_fusion.1
  19.1 3.7 fusion.50
  23.1 44.6 %all_gather.15 = bf16[4,6,1152]{1,0,2:T(4,128)(2,1)} all-gather(bf16[4,6,288]{1,0,2:T(4,128)(2,1)S(1)} %copy.105), channel_id=1, replica_groups=mesh['dp'=8,'tensor'=4] {'tensor'}, dimensions={2}, use_global_device_ids=true | all-gather | bytes 69120 | tf_op jit(solution)/shard_map/all_gather | solution.py:110
  67.7 2.0 copy.106
  70.1 11.2 %all-gather.5.cloned.1.call-done = bf16[4,256,1152]{2,1,0:T(8,128)(2,1)} async-done(((bf16[1,256,1152]{2,1,0:T(8,128)(2,1)}), bf16[4,256,1152]{2,1,0:T(8,128)(2,1)}) %all-gather.5.cloned.1.call-update) | async-done | bytes 2359312 | tf_op jit(solution)/shard_map/all_gather | solution.py:109
  81.3 2.2 convert_reduce_fusion
  85.1 2.7 fusion.18
  90.7 1.2 multiply_reduce_fusion.1
  92.7 1.3 copy-done.1
  95.7 2.9 convolution_convert_fusion.1
  98.8 1.3 convert_element_type.262
  100.1 1.5 fusion.70
  101.6 43.7 %reduce-scatter.13.cloned.1.call-done = bf16[1,256,1152]{2,1,0:T(8,128)(2,1)} async-done(((bf16[4,256,1152]{2,1,0:T(8,128)(2,1)}), bf16[1,256,1152]{2,1,0:T(8,128)(2,1)}) %reduce-scatter.13.cloned.1.call-update) | async-done | bytes 589840 | tf_op jit(solution)/shard_map/reduce_scatter | solution.py:139
  145.3 1.4 fusion.96
  148.4 1.2 add_convert_fusion
  150.4 2.7 convert_reduce_fusion.4
  153.1 46.1 %all-gather.7.cloned.1.call-done = bf16[4,256,1152]{2,1,0:T(8,128)(2,1)} async-done(((bf16[1,256,1152]{2,1,0:T(8,128)(2,1)}), bf16[4,256,1152]{2,1,0:T(8,128)(2,1)}) %all-gather.7.cloned.1.call-update) | async-done | bytes 2359312 | tf_op jit(solution)/shard_map/all_gather | solution.py:152
  199.2 9.6 fusion.7
  208.8 41.2 %all-gather.9.cloned.1.call-done = bf16[4,256,1152]{2,1,0:T(8,128)(2,1)} async-done(((bf16[1,256,1152]{2,1,0:T(8,128)(2,1)}), bf16[4,256,1152]{2,1,0:T(8,128)(2,1)}) %all-gather.9.cloned.1.call-update) | async-done | bytes 2359312 | tf_op jit(solution)/shard_map/all_gather | solution.py:172
  250.0 8.4 fusion.30
  258.4 1.2 copy-done.87
  260.0 5.5 bitcast_convert_fusion.1
  265.6 5.6 convolution_convert_fusion
  271.5 1.3 convert_element_type.267
  272.8 39.4 %reduce-scatter.17.cloned.1.call-done = bf16[1,256,1152]{2,1,0:T(8,128)(2,1)} async-done(((bf16[4,256,1152]{2,1,0:T(8,128)(2,1)}), bf16[1,256,1152]{2,1,0:T(8,128)(2,1)}) %reduce-scatter.17.cloned.1.call-update) | async-done | bytes 589840 | tf_op jit(solution)/shard_map/reduce_scatter | solution.py:184
  312.2 2.8 fusion.46
  316.7 44.8 %reduce-scatter.15.cloned.1.call-done = bf16[1,256,1152]{2,1,0:T(8,128)(2,1)} async-done(((bf16[4,256,1152]{2,1,0:T(8,128)(2,1)}), bf16[1,256,1152]{2,1,0:T(8,128)(2,1)}) %reduce-scatter.15.cloned.1.call-update) | async-done | bytes 589840 | tf_op jit(solution)/shard_map/reduce_scatter | solution.py:160
  361.5 4.4 multiply_reduce_fusion.3
  366.9 1.5 convert_reduce_fusion.5
  368.5 49.5 %all-gather.11.cloned.1.call-done = bf16[4,256,1152]{2,1,0:T(8,128)(2,1)} async-done(((bf16[1,256,1152]{2,1,0:T(8,128)(2,1)}), bf16[4,256,1152]{2,1,0:T(8,128)(2,1)}) %all-gather.11.cloned.1.call-update) | async-done | bytes 2359312 | tf_op jit(solution)/shard_map/all_gather | solution.py:197
  418.0 2.9 convolution_convert_fusion.3
  421.9 2.6 multiply_reduce_fusion
  428.2 1.1 copy-done.7
  430.9 1.3 copy-done.5
  435.0 4.1 bitcast_convert_fusion
  439.6 9.4 convolution_bitcast_fusion
  449.1 5.9 convolution_bitcast_fusion.2
  455.1 4.6 convolution_bitcast_fusion.3
  460.4 8.2 convolution_bitcast_fusion.1
  469.4 16.4 %reduce-scatter.19.cloned.1.call-done = bf16[1,256,1152]{2,1,0:T(8,128)(2,1)} async-done(((bf16[4,256,1152]{2,1,0:T(8,128)(2,1)}), bf16[1,256,1152]{2,1,0:T(8,128)(2,1)}) %reduce-scatter.19.cloned.1.call-update) | async-done | bytes 589840 | tf_op jit(solution)/shard_map/reduce_scatter | solution.py:236
  485.8 2.2 fusion.49
  488.1 1.3 copy.125
  489.9 7.7 reduce.24
  498.6 8.8 all_to_all.4
  507.4 1.4 reshape.415
  508.8 1.3 copy.126
  510.2 2.8 convolution_bitcast_fusion.4
  513.0 16.3 %psum.47 = f32[4,1152]{1,0:T(4,128)S(1)} all-reduce(f32[4,1152]{1,0:T(4,128)S(1)} %convolution_bitcast_fusion.4), channel_id=1, replica_groups=mesh['dp'=8,'tensor'=4] {'tensor'}, use_global_device_ids=true, to_apply=%region_42.43 | all-reduce | flops 4608 | bytes 36864 | tf_op jit(solution)/shard_map/psum | solution.py:266
  530.2 1.4 fusion.79
  531.7 3.0 fusion.65
  534.7 3.3 fusion.95
  538.1 5.7 fusion.63
  545.7 8.4 reduce-scatter.25.cloned.1.call-done
  554.1 2.9 copy.127
  557.1 1.3 fusion.39
  558.4 22.9 %all-reduce.15 = (f32[1152]{0:T(1024)S(1)}, f32[1152]{0:T(1024)S(1)}) all-reduce(f32[1152]{0:T(1024)S(1)} %get-tuple-element.164, f32[1152]{0:T(1024)S(1)} %get-tuple-element.110), channel_id=12, replica_groups=mesh['dp'=8,'tensor'=4] {'dp'}, use_global_device_ids=true, to_apply=%region_45.46.clone | all-reduce | flops 2304 | bytes 18432
  583.0 40.9 %all-reduce.14 = (f32[72]{0:T(128)}, f32[72]{0:T(128)}, f32[1152]{0:T(1024)}, f32[1152]{0:T(1024)}, f32[6,1152]{1,0:T(8,128)}) all-reduce(f32[72]{0:T(128)S(1)} %copy-done.80, f32[72]{0:T(128)S(1)} %copy-done.79, f32[1152]{0:T(1024)S(1)} %copy-done.51, f32[1152]{0:T(1024)S(1)} %copy-done.50, ...), channel_id=1, replica_groups=mesh['dp'=8,'tensor'=4] {'dp','tensor'}, use_global_device_ids=true, to_apply=%region_23.24 | all-reduce | flops 9360 | bytes 74880 | tf_op jit(solution)/shard_map/psum | solution.py:277
  623.8 25.9 %reduce-scatter.23.cloned.1.call-done = f32[288,144]{0,1:T(8,128)} async-done(((f32[288,1152]{0,1:T(8,128)}), f32[288,144]{0,1:T(8,128)}) %reduce-scatter.23.cloned.1.call-update) | async-done | bytes 165904 | tf_op jit(solution)/shard_map/reduce_scatter | solution.py:303
  649.8 60.7 %reduce-scatter.21.cloned.1.call-done = f32[144,3,288]{2,0,1:T(8,128)} async-done(((f32[1152,3,288]{2,0,1:T(8,128)}), f32[144,3,288]{2,0,1:T(8,128)}) %reduce-scatter.21.cloned.1.call-update) | async-done | bytes 497680 | tf_op jit(solution)/shard_map/reduce_scatter | solution.py:302
  710.4 40.5 %reduce-scatter.31.cloned.1.call-done = f32[256,144]{0,1:T(8,128)} async-done(((f32[256,1152]{0,1:T(8,128)}), f32[256,144]{0,1:T(8,128)}) %reduce-scatter.31.cloned.1.call-update) | async-done | bytes 147472 | tf_op jit(solution)/shard_map/reduce_scatter | solution.py:308
  750.9 57.7 %reduce-scatter.35.cloned.1.call-done = f32[1000,144]{0,1:T(8,128)} async-done(((f32[1000,1152]{0,1:T(8,128)}), f32[1000,144]{0,1:T(8,128)}) %reduce-scatter.35.cloned.1.call-update) | async-done | bytes 576016 | tf_op jit(solution)/shard_map/reduce_scatter | solution.py:306
  808.6 60.7 %reduce-scatter.33.cloned.1.call-done = f32[144,1152]{1,0:T(8,128)} async-done(((f32[1152,1152]{1,0:T(8,128)}), f32[144,1152]{1,0:T(8,128)}) %reduce-scatter.33.cloned.1.call-update) | async-done | bytes 663568 | tf_op jit(solution)/shard_map/reduce_scatter | solution.py:310
  869.4 86.3 %reduce-scatter.29.cloned.1.call-done = f32[144,6,288]{2,0,1:T(8,128)} async-done(((f32[1152,6,288]{2,0,1:T(8,128)}), f32[144,6,288]{2,0,1:T(8,128)}) %reduce-scatter.29.cloned.1.call-update) | async-done | bytes 995344 | tf_op jit(solution)/shard_map/reduce_scatter | solution.py:307
  (282 shorter events, 37.3 us)
Async XLA Ops:
  7.2 10.7 %copy-start = (bf16[1152,1152]{1,0:T(8,128)(2,1)S(1)}, bf16[1152,1152]{1,0:T(8,128)(2,1)}, u32[]{:S(2)}) copy-start(bf16[1152,1152]{1,0:T(8,128)(2,1)} %param.37) | copy-start | bytes 7962628
  7.2 74.1 %all-gather.5.cloned.1.call-start = ((), (), s32[]{:S(2)}) async-start(), calls=%async_computation.13 | async-start | bytes 2949120 | tf_op jit(solution)/shard_map/all_gather | solution.py:109
  7.9 137.3 %reduce-scatter.13.cloned.1.call-start = ((), (), s32[]{:S(2)}) async-start(), calls=%async_computation.14 | async-start | bytes 2949120 | tf_op jit(solution)/shard_map/reduce_scatter | solution.py:139
  8.7 79.7 %copy-start.70 = (f32[72]{0:T(128)}, f32[72]{0:T(128)S(1)}, u32[]{:S(2)}) copy-start(f32[72]{0:T(128)S(1)} %convert_element_type.252) | copy-start | bytes 868
  9.3 79.3 %copy-start.72 = (f32[72]{0:T(128)}, f32[72]{0:T(128)S(1)}, u32[]{:S(2)}) copy-start(f32[72]{0:T(128)S(1)} %convert_element_type.255) | copy-start | bytes 868
  69.7 14.7 %copy-start.39 = (f32[4,6,1152]{2,0,1:T(4,128)}, f32[4,6,1152]{2,0,1:T(4,128)S(1)}, u32[]{:S(2)}) copy-start(f32[4,6,1152]{2,0,1:T(4,128)S(1)} %convert_element_type.248) | copy-start | bytes 331780
  70.1 14.4 %copy-start.54 = (f32[4,1152]{1,0:T(4,128)}, f32[4,1152]{1,0:T(4,128)S(1)}, u32[]{:S(2)}) copy-start(f32[4,1152]{1,0:T(4,128)S(1)} %get-tuple-element.150) | copy-start | bytes 55300
  70.1 14.4 %copy-start.56 = (f32[4,1152]{1,0:T(4,128)}, f32[4,1152]{1,0:T(4,128)S(1)}, u32[]{:S(2)}) copy-start(f32[4,1152]{1,0:T(4,128)S(1)} %get-tuple-element.151) | copy-start | bytes 55300
  81.3 2.4 copy-start.11
  83.5 1.6 copy-start.83
  83.7 4.1 copy-start.58
  84.4 3.4 copy-start.76
  87.8 4.9 copy-start.12
  88.1 1.6 copy-start.6
  88.3 1.5 copy-start.44
  88.3 1.5 copy-start.46
  88.4 1.5 copy-start.42
  88.4 1.5 copy-start.40
  90.2 1.6 copy-start.14
  90.3 1.6 copy-start.16
  90.3 1.6 copy-start.18
  91.9 2.0 copy-start.1
  94.0 1.7 copy-start.85
  98.6 46.7 %copy-start.3 = (bf16[1,256,1152]{2,1,0:T(8,128)(2,1)S(1)}, bf16[1,256,1152]{2,1,0:T(8,128)(2,1)}, u32[]{:S(2)}) copy-start(bf16[1,256,1152]{2,1,0:T(8,128)(2,1)} %param.20) | copy-start | bytes 1769476
  98.6 100.6 %all-gather.7.cloned.1.call-start = ((), (), s32[]{:S(2)}) async-start(), calls=%async_computation.15 | async-start | bytes 2949120 | tf_op jit(solution)/shard_map/all_gather | solution.py:152
  145.3 3.2 copy-start.32
  145.3 3.2 copy-start.34
  145.3 3.2 copy-start.48
  145.3 3.2 copy-start.52
  149.7 100.3 %all-gather.9.cloned.1.call-start = ((), (), s32[]{:S(2)}) async-start(), calls=%async_computation.17 | async-start | bytes 2949120 | tf_op jit(solution)/shard_map/all_gather | solution.py:172
  153.1 159.1 %reduce-scatter.17.cloned.1.call-start = ((), (), s32[]{:S(2)}) async-start(), calls=%async_computation.18 | async-start | bytes 2949120 | tf_op jit(solution)/shard_map/reduce_scatter | solution.py:184
  250.0 10.0 %copy-start.82 = (bf16[1152,2,768]{2,1,0:T(2,128)(2,1)S(1)}, bf16[1152,2,768]{2,1,0:T(2,128)(2,1)}, u32[]{:S(2)}) copy-start(bf16[1152,2,768]{2,1,0:T(2,128)(2,1)} %param.30) | copy-start | bytes 10616836
  258.4 1.7 copy-start.88
  265.6 95.9 %reduce-scatter.15.cloned.1.call-start = ((), (), s32[]{:S(2)}) async-start(), calls=%async_computation.16 | async-start | bytes 2949120 | tf_op jit(solution)/shard_map/reduce_scatter | solution.py:160
  271.2 146.7 %all-gather.11.cloned.1.call-start = ((), (), s32[]{:S(2)}) async-start(), calls=%async_computation.19 | async-start | bytes 2949120 | tf_op jit(solution)/shard_map/all_gather | solution.py:197
  361.5 5.4 copy-start.33
  368.5 117.3 %reduce-scatter.19.cloned.1.call-start = ((), (), s32[]{:S(2)}) async-start(), calls=%async_computation.20 | async-start | bytes 2949120 | tf_op jit(solution)/shard_map/reduce_scatter | solution.py:236
  418.0 3.1 copy-start.2
  421.9 11.8 %copy-start.31 = (bf16[4,4,72,256]{3,2,1,0:T(8,128)(2,1)}, bf16[4,4,72,256]{3,2,1,0:T(8,128)(2,1)S(1)}, u32[]{:S(2)}) copy-start(bf16[4,4,72,256]{3,2,1,0:T(8,128)(2,1)S(1)} %convolution_convert_fusion.2) | copy-start | bytes 1769476
  430.7 3.0 copy-start.29
  433.3 1.8 copy-start.84
  439.2 115.0 %reduce-scatter.25.cloned.1.call-start = ((), (), s32[]{:S(2)}) async-start(), calls=%async_computation.23 | async-start | bytes 7962624 | tf_op jit(solution)/shard_map/reduce_scatter | solution.py:304
  449.1 174.8 %reduce-scatter.27.cloned.1.call-start = ((), (), s32[]{:S(2)}) async-start(), calls=%async_computation.24 | async-start | bytes 3981312 | tf_op jit(solution)/shard_map/reduce_scatter | solution.py:305
  455.1 194.7 %reduce-scatter.23.cloned.1.call-start = ((), (), s32[]{:S(2)}) async-start(), calls=%async_computation.22 | async-start | bytes 1990656 | tf_op jit(solution)/shard_map/reduce_scatter | solution.py:303
  459.7 250.7 %reduce-scatter.21.cloned.1.call-start = ((), (), s32[]{:S(2)}) async-start(), calls=%async_computation.21 | async-start | bytes 5971968 | tf_op jit(solution)/shard_map/reduce_scatter | solution.py:302
  468.6 17.2 %copy-start.49 = (f32[1152]{0:T(1024)S(1)}, f32[1152]{0:T(1024)}, u32[]{:S(2)}) copy-start(f32[1152]{0:T(1024)} %get-tuple-element.98) | copy-start | bytes 13828
  468.6 17.2 %copy-start.64 = (f32[256]{0:T(256)S(1)}, f32[256]{0:T(256)}, u32[]{:S(2)}) copy-start(f32[256]{0:T(256)} %broadcast_multiply_fusion.3) | copy-start | bytes 3076
  468.7 282.3 %reduce-scatter.31.cloned.1.call-start = ((), (), s32[]{:S(2)}) async-start(), calls=%async_computation.26 | async-start | bytes 1327104 | tf_op jit(solution)/shard_map/reduce_scatter | solution.py:308
  510.2 19.1 %copy-start.36 = (f32[4,1152]{1,0:T(4,128)S(1)}, f32[4,1152]{1,0:T(4,128)}, u32[]{:S(2)}) copy-start(f32[4,1152]{1,0:T(4,128)} %copy-done.35) | copy-start | bytes 55300
  510.2 19.1 %copy-start.38 = (f32[4,1152]{1,0:T(4,128)S(1)}, f32[4,1152]{1,0:T(4,128)}, u32[]{:S(2)}) copy-start(f32[4,1152]{1,0:T(4,128)} %copy-done.37) | copy-start | bytes 55300
  513.0 17.2 %copy-start.67 = (bf16[4,128]{1,0:T(4,128)(2,1)S(1)}, bf16[4,128]{1,0:T(4,128)(2,1)}, u32[]{:S(2)}) copy-start(bf16[4,128]{1,0:T(4,128)(2,1)} %copy-done.66) | copy-start | bytes 3076
  513.0 17.2 %copy-start.69 = (bf16[4,128]{1,0:T(4,128)(2,1)S(1)}, bf16[4,128]{1,0:T(4,128)(2,1)}, u32[]{:S(2)}) copy-start(bf16[4,128]{1,0:T(4,128)(2,1)} %copy-done.68) | copy-start | bytes 3076
  530.2 1.5 copy-start.81
  531.6 277.0 %reduce-scatter.35.cloned.1.call-start = ((), (), s32[]{:S(2)}) async-start(), calls=%async_computation.28 | async-start | bytes 5308416 | tf_op jit(solution)/shard_map/reduce_scatter | solution.py:306
  534.7 334.7 %reduce-scatter.33.cloned.1.call-start = ((), (), s32[]{:S(2)}) async-start(), calls=%async_computation.27 | async-start | bytes 5971968 | tf_op jit(solution)/shard_map/reduce_scatter | solution.py:310
  538.1 417.6 %reduce-scatter.29.cloned.1.call-start = ((), (), s32[]{:S(2)}) async-start(), calls=%async_computation.25 | async-start | bytes 11943936 | tf_op jit(solution)/shard_map/reduce_scatter | solution.py:307
  543.9 13.2 %copy-start.75 = (f32[256]{0:T(256)S(1)}, f32[256]{0:T(256)}, u32[]{:S(2)}) copy-start(f32[256]{0:T(256)} %get-tuple-element.92) | copy-start | bytes 3076
  543.9 13.2 %copy-start.74 = (f32[256]{0:T(256)S(1)}, f32[256]{0:T(256)}, u32[]{:S(2)}) copy-start(f32[256]{0:T(256)} %get-tuple-element.93) | copy-start | bytes 3076
  554.1 3.0 copy-start.10
  554.1 3.0 copy-start.13
  557.0 25.9 %copy-start.50 = (f32[1152]{0:T(1024)S(1)}, f32[1152]{0:T(1024)}, u32[]{:S(2)}) copy-start(f32[1152]{0:T(1024)} %get-tuple-element.114) | copy-start | bytes 13828
  557.0 25.9 %copy-start.51 = (f32[1152]{0:T(1024)S(1)}, f32[1152]{0:T(1024)}, u32[]{:S(2)}) copy-start(f32[1152]{0:T(1024)} %get-tuple-element.116) | copy-start | bytes 13828
  557.0 25.9 %copy-start.79 = (f32[72]{0:T(128)S(1)}, f32[72]{0:T(128)}, u32[]{:S(2)}) copy-start(f32[72]{0:T(128)} %get-tuple-element.85) | copy-start | bytes 868
  557.0 25.9 %copy-start.80 = (f32[72]{0:T(128)S(1)}, f32[72]{0:T(128)}, u32[]{:S(2)}) copy-start(f32[72]{0:T(128)} %get-tuple-element.87) | copy-start | bytes 868
  (41 other events, 40.9 us)
Sparse Core Ops, SparseCore 0:
  9.6 71.6 all-gather.4
  98.7 46.4 reduce-scatter.12
  149.8 49.3 all-gather.6
  201.2 48.7 all-gather.8
  265.7 46.4 reduce-scatter.16
  314.4 47.0 reduce-scatter.14
  368.6 49.3 all-gather.10
  439.3 46.4 reduce-scatter.18
  489.3 64.7 reduce-scatter.24
  558.0 48.4 reduce-scatter.26
  610.5 39.2 reduce-scatter.22
  653.6 56.7 reduce-scatter.20
  714.2 36.6 reduce-scatter.30
  754.8 53.7 reduce-scatter.34
  812.5 56.8 reduce-scatter.32
  873.3 82.3 reduce-scatter.28
where the time goes:
time: 972 us; the launch traced here: 962 us
  waiting for transfers between devices  633 us (65%)
  blocking collectives  133 us (14%)
  matrix products  99 us (10%)
  other arithmetic  47.9 us (5%)
  local copies, waits for them, and re-layouts  30.4 us (3%)
  between operations  16.6 us (2%)
    reduce_scatter x1, waiting for transfers between devices, shards(): lax.psum_scatter(modulate_local, 'dp', scatter_dimension=0, tiled=True)  86.3 us
    reduce_scatter x1, waiting for transfers between devices, shards(): lax.psum_scatter(embed_local, 'dp', scatter_dimension=0, tiled=True)  60.7 us
    reduce_scatter x1, waiting for transfers between devices, shards(): lax.psum_scatter(project_grad, 'dp', scatter_dimension=0, tiled=True)  60.7 us
    reduce_scatter x1, waiting for transfers between devices, shards(): lax.psum_scatter(class_grad, 'dp', scatter_dimension=1, tiled=True)  57.7 us
    all_gather x1, waiting for transfers between devices, shards(): piece = lax.all_gather(attend_grad, 'tensor', axis=0, tiled=True)  49.5 us
    all_gather x1, waiting for transfers between devices, shards(): mod_two_all = lax.all_gather(mod_two, 'tensor', axis=0, tiled=True)  46.1 us
    reduce_scatter x1, waiting for transfers between devices, shards(): lax.psum_scatter(jnp.einsum('blf,fd->bld', piece, down_weight, preferred_...  44.8 us
    all_gather x1, blocking collectives, shards(): lax.all_gather(modulation_part, 'tensor', axis=2, tiled=True)  44.6 us
  transfers between devices with their start and end apart: 16, of which 15 were waited for; matrix products, arithmetic and copies ran while one was open for 11% of the time, Pallas kernels for 0%

commit v1 on v0

--- a/solution.py
+++ b/solution.py
@@ -8,6 +8,18 @@
 FREQ = 256
 GRID = 16
 EPS = 1e-06
+
+
+def gather_by_bits(shard, axis, dim):
+    ways, here = (lax.axis_size(axis), lax.axis_index(axis))
+    grown, reach = (shard, 1)
+    while reach < ways:
+        theirs = lax.ppermute(grown, axis, [(d, d ^ reach) for d in range(ways)])
+        mine_first = jnp.concatenate([grown, theirs], axis=dim)
+        theirs_first = jnp.concatenate([theirs, grown], axis=dim)
+        grown = jnp.where(here & reach == 0, mine_first, theirs_first)
+        reach = 2 * reach
+    return grown
 
 
 def layer_norm(value):
@@ -149,7 +161,7 @@
     residual = token_local + attend_gate * attend_branch
     normed_two, inverse_two = layer_norm(residual)
     mod_two = (normed_two * (1.0 + feed_scale) + feed_shift).astype(jnp.bfloat16)
-    mod_two_all = lax.all_gather(mod_two, "tensor", axis=0, tiled=True)
+    mod_two_all = gather_by_bits(mod_two, "tensor", 0)
     gate_up = jnp.einsum(
         "bld,dkf->blkf", mod_two_all, expand_weight, preferred_element_type=jnp.float32
     )

time: 972 us -> 982 us (1.010)
    ppermute x0 -> x2, waiting for transfers between devices: none -> 95.6 us  [gather_by_bits(): theirs = lax.ppermute(grown, axis, [(d, d ^ reach) for d in range(ways)])]
    all_gather x1 -> x0, waiting for transfers between devices: 46.1 us -> none  [shards(): mod_two_all = lax.all_gather(mod_two, 'tensor', axis=0, tiled=True)]
    all_gather x1, waiting for transfers between devices: 41.2 us -> 0.01 us  [shards(): piece = lax.all_gather(branch_grad, 'tensor', axis=0, tiled=True)]
    unnamed x185 -> x187, local copies, waits for them, and re-layouts: 22.2 us -> 21.7 us
  transfers between devices with their start and end apart: 16 -> 17, of which waited for: 15 -> 15; matrix products, arithmetic and copies ran while one was open for 11% -> 12% of each run, Pallas kernels for 0% -> 0%
where the time goes in v1:
time: 982 us; the launch traced here: 972 us
  waiting for transfers between devices  637 us (65%)
  blocking collectives  133 us (14%)
  matrix products  101 us (10%)
  other arithmetic  50.7 us (5%)
  local copies, waits for them, and re-layouts  29.8 us (3%)
  between operations  16.7 us (2%)
    ppermute x2, waiting for transfers between devices, gather_by_bits(): theirs = lax.ppermute(grown, axis, [(d, d ^ reach) for d in range(ways)])  95.6 us
    reduce_scatter x1, waiting for transfers between devices, shards(): lax.psum_scatter(modulate_local, 'dp', scatter_dimension=0, tiled=True)  86.3 us
    reduce_scatter x1, waiting for transfers between devices, shards(): lax.psum_scatter(project_grad, 'dp', scatter_dimension=0, tiled=True)  60.8 us
    reduce_scatter x1, waiting for transfers between devices, shards(): lax.psum_scatter(embed_local, 'dp', scatter_dimension=0, tiled=True)  60.7 us
    reduce_scatter x1, waiting for transfers between devices, shards(): lax.psum_scatter(class_grad, 'dp', scatter_dimension=1, tiled=True)  57.8 us
    all_gather x1, waiting for transfers between devices, shards(): piece = lax.all_gather(attend_grad, 'tensor', axis=0, tiled=True)  49.5 us
    reduce_scatter x1, waiting for transfers between devices, shards(): lax.psum_scatter(jnp.einsum('blf,fd->bld', piece, down_weight, preferred_...  44.8 us
    all_gather x1, blocking collectives, shards(): lax.all_gather(modulation_part, 'tensor', axis=2, tiled=True)  44.6 us
  transfers between devices with their start and end apart: 17, of which 15 were waited for; matrix products, arithmetic and copies ran while one was open for 12% of the time, Pallas kernels for 0%

profile of v1, /device:TPU:0, one launch (start us, length us, event | category | flops | bytes accessed | tf_op | source)
XLA Modules:
  0.0 972.3 jit_solution(3821256327253653584)
XLA Ops:
  12.7 2.5 gather_fusion
  16.6 1.3 convolution_add_fusion.1
  19.1 3.7 fusion.50
  23.0 44.6 %all_gather.12 = bf16[4,6,1152]{1,0,2:T(4,128)(2,1)} all-gather(bf16[4,6,288]{1,0,2:T(4,128)(2,1)S(1)} %copy.105), channel_id=1, replica_groups=mesh['dp'=8,'tensor'=4] {'tensor'}, dimensions={2}, use_global_device_ids=true | all-gather | bytes 69120 | tf_op jit(solution)/shard_map/all_gather | solution.py:122
  67.7 2.0 copy.106
  70.1 11.3 %all-gather.4.cloned.1.call-done = bf16[4,256,1152]{2,1,0:T(8,128)(2,1)} async-done(((bf16[1,256,1152]{2,1,0:T(8,128)(2,1)}), bf16[4,256,1152]{2,1,0:T(8,128)(2,1)}) %all-gather.4.cloned.1.call-update) | async-done | bytes 2359312 | tf_op jit(solution)/shard_map/all_gather | solution.py:121
  81.3 2.2 convert_reduce_fusion
  85.1 2.7 fusion.18
  90.8 1.2 multiply_reduce_fusion.1
  92.8 1.3 copy-done.1
  95.2 3.0 convolution_convert_fusion.1
  98.9 1.5 fusion.70
  101.0 2.6 convert_reduce_fusion.4
  103.9 1.3 convert_element_type.262
  105.2 39.6 %reduce-scatter.13.cloned.1.call-done = bf16[1,256,1152]{2,1,0:T(8,128)(2,1)} async-done(((bf16[4,256,1152]{2,1,0:T(8,128)(2,1)}), bf16[1,256,1152]{2,1,0:T(8,128)(2,1)}) %reduce-scatter.13.cloned.1.call-update) | async-done | bytes 589840 | tf_op jit(solution)/shard_map/reduce_scatter | solution.py:151
  144.8 1.4 fusion.97
  147.4 1.2 add_convert_fusion
  149.5 36.5 %collective-permute-done = bf16[1,256,1152]{2,1,0:T(8,128)(2,1)} collective-permute-done((bf16[1,256,1152]{2,1,0:T(8,128)(2,1)}, bf16[1,256,1152]{2,1,0:T(8,128)(2,1)}, u32[]{:S(2)}, u32[]{:S(2)}) %collective-permute-start) | collective-permute-done | bytes 589856 | tf_op jit(solution)/shard_map/ppermute | solution.py:17
  186.0 2.9 maximum_select_fusion.1
  188.9 1.3 collective-permute-start.1
  190.2 59.1 %collective-permute-done.1 = bf16[2,256,1152]{2,1,0:T(8,128)(2,1)} collective-permute-done((bf16[2,256,1152]{2,1,0:T(8,128)(2,1)}, bf16[2,256,1152]{2,1,0:T(8,128)(2,1)}, u32[]{:S(2)}, u32[]{:S(2)}) %collective-permute-start.1) | collective-permute-done | bytes 1179680 | tf_op jit(solution)/shard_map/ppermute | solution.py:17
  249.3 10.4 %fusion.7 = f32[4,256,2,768]{3,1,2,0:T(8,128)} fusion(bf16[1152,2,768]{2,1,0:T(2,128)(2,1)} %param.30, bf16[2,256,1152]{2,1,0:T(8,128)(2,1)} %collective-permute-done.1, bf16[2,256,1152]{2,1,0:T(8,128)(2,1)} %maximum_select_fusion.1, pred[]{:T(512)S(6)} %eq.24), kind=kOutput, calls=%fused_computation.22 | convolution fusion | flops 3634495488 | bytes 12189697 | tf_op jit(solution)/shard_map/bld,dkf->blkf/dot_general | solution.py:165
  259.7 8.4 fusion.30
  269.8 5.5 bitcast_convert_fusion.1
  275.4 5.6 convolution_convert_fusion
  281.3 1.3 convert_element_type.267
  282.6 39.5 %reduce-scatter.17.cloned.1.call-done = bf16[1,256,1152]{2,1,0:T(8,128)(2,1)} async-done(((bf16[4,256,1152]{2,1,0:T(8,128)(2,1)}), bf16[1,256,1152]{2,1,0:T(8,128)(2,1)}) %reduce-scatter.17.cloned.1.call-update) | async-done | bytes 589840 | tf_op jit(solution)/shard_map/reduce_scatter | solution.py:196
  322.0 2.8 fusion.46
  326.5 44.8 %reduce-scatter.15.cloned.1.call-done = bf16[1,256,1152]{2,1,0:T(8,128)(2,1)} async-done(((bf16[4,256,1152]{2,1,0:T(8,128)(2,1)}), bf16[1,256,1152]{2,1,0:T(8,128)(2,1)}) %reduce-scatter.15.cloned.1.call-update) | async-done | bytes 589840 | tf_op jit(solution)/shard_map/reduce_scatter | solution.py:172
  371.3 4.4 multiply_reduce_fusion.3
  376.7 1.5 convert_reduce_fusion.5
  378.3 49.5 %all-gather.8.cloned.1.call-done = bf16[4,256,1152]{2,1,0:T(8,128)(2,1)} async-done(((bf16[1,256,1152]{2,1,0:T(8,128)(2,1)}), bf16[4,256,1152]{2,1,0:T(8,128)(2,1)}) %all-gather.8.cloned.1.call-update) | async-done | bytes 2359312 | tf_op jit(solution)/shard_map/all_gather | solution.py:209
  427.7 2.9 convolution_convert_fusion.3
  431.7 2.6 multiply_reduce_fusion
  440.7 1.3 copy-done.5
  444.8 4.1 bitcast_convert_fusion
  449.4 10.2 %convolution_bitcast_fusion = f32[1152,2,768]{2,0,1:T(8,128)} fusion(bf16[4,256,1,768]{3,1,0,2:T(8,128)(2,1)} %copy-done.89, bf16[4,256,1,768]{3,1,0,2:T(8,128)(2,1)} %copy-done.88, bf16[2,256,1152]{2,1,0:T(8,128)(2,1)} %collective-permute-done.1, bf16[2,256,1152]{2,1,0:T(8,128)(2,1)} %maximum_select_fusion.1, pred[]{:T(512)S(6)} %eq.24), kind=kOutput, calls=%fused_computation.5 | convolution fusion | flops 3640786944 | bytes 12582913 | tf_op jit(solution)/shard_map/bld,blkf->dkf/dot_general | solution.py:192
  459.7 6.0 convolution_bitcast_fusion.2
  465.7 4.6 convolution_bitcast_fusion.3
  471.0 8.1 convolution_bitcast_fusion.1
  480.0 15.6 %reduce-scatter.19.cloned.1.call-done = bf16[1,256,1152]{2,1,0:T(8,128)(2,1)} async-done(((bf16[4,256,1152]{2,1,0:T(8,128)(2,1)}), bf16[1,256,1152]{2,1,0:T(8,128)(2,1)}) %reduce-scatter.19.cloned.1.call-update) | async-done | bytes 589840 | tf_op jit(solution)/shard_map/reduce_scatter | solution.py:248
  495.6 2.2 fusion.49
  497.9 1.3 copy.125
  499.7 7.7 reduce.24
  508.3 8.8 all_to_all.4
  517.2 1.4 reshape.415
  518.5 1.3 copy.126
  520.0 2.8 convolution_bitcast_fusion.4
  522.8 16.3 %psum.47 = f32[4,1152]{1,0:T(4,128)S(1)} all-reduce(f32[4,1152]{1,0:T(4,128)S(1)} %convolution_bitcast_fusion.4), channel_id=1, replica_groups=mesh['dp'=8,'tensor'=4] {'tensor'}, use_global_device_ids=true, to_apply=%region_42.43 | all-reduce | flops 4608 | bytes 36864 | tf_op jit(solution)/shard_map/psum | solution.py:278
  540.0 1.4 fusion.79
  541.5 3.0 fusion.65
  544.5 3.3 fusion.96
  547.9 5.7 fusion.63
  555.5 8.4 reduce-scatter.25.cloned.1.call-done
  563.9 2.9 copy.127
  566.9 1.3 fusion.39
  568.2 22.9 %all-reduce.15 = (f32[1152]{0:T(1024)S(1)}, f32[1152]{0:T(1024)S(1)}) all-reduce(f32[1152]{0:T(1024)S(1)} %get-tuple-element.164, f32[1152]{0:T(1024)S(1)} %get-tuple-element.110), channel_id=12, replica_groups=mesh['dp'=8,'tensor'=4] {'dp'}, use_global_device_ids=true, to_apply=%region_45.46.clone | all-reduce | flops 2304 | bytes 18432
  592.8 40.8 %all-reduce.14 = (f32[72]{0:T(128)}, f32[72]{0:T(128)}, f32[1152]{0:T(1024)}, f32[1152]{0:T(1024)}, f32[6,1152]{1,0:T(8,128)}) all-reduce(f32[72]{0:T(128)S(1)} %copy-done.81, f32[72]{0:T(128)S(1)} %copy-done.80, f32[1152]{0:T(1024)S(1)} %copy-done.52, f32[1152]{0:T(1024)S(1)} %copy-done.51, ...), channel_id=1, replica_groups=mesh['dp'=8,'tensor'=4] {'dp','tensor'}, use_global_device_ids=true, to_apply=%region_23.24 | all-reduce | flops 9360 | bytes 74880 | tf_op jit(solution)/shard_map/psum | solution.py:289
  633.6 26.0 %reduce-scatter.23.cloned.1.call-done = f32[288,144]{0,1:T(8,128)} async-done(((f32[288,1152]{0,1:T(8,128)}), f32[288,144]{0,1:T(8,128)}) %reduce-scatter.23.cloned.1.call-update) | async-done | bytes 165904 | tf_op jit(solution)/shard_map/reduce_scatter | solution.py:315
  659.5 60.8 %reduce-scatter.21.cloned.1.call-done = f32[144,3,288]{2,0,1:T(8,128)} async-done(((f32[1152,3,288]{2,0,1:T(8,128)}), f32[144,3,288]{2,0,1:T(8,128)}) %reduce-scatter.21.cloned.1.call-update) | async-done | bytes 497680 | tf_op jit(solution)/shard_map/reduce_scatter | solution.py:314
  720.4 40.4 %reduce-scatter.31.cloned.1.call-done = f32[256,144]{0,1:T(8,128)} async-done(((f32[256,1152]{0,1:T(8,128)}), f32[256,144]{0,1:T(8,128)}) %reduce-scatter.31.cloned.1.call-update) | async-done | bytes 147472 | tf_op jit(solution)/shard_map/reduce_scatter | solution.py:320
  760.7 57.8 %reduce-scatter.35.cloned.1.call-done = f32[1000,144]{0,1:T(8,128)} async-done(((f32[1000,1152]{0,1:T(8,128)}), f32[1000,144]{0,1:T(8,128)}) %reduce-scatter.35.cloned.1.call-update) | async-done | bytes 576016 | tf_op jit(solution)/shard_map/reduce_scatter | solution.py:318
  818.6 60.7 %reduce-scatter.33.cloned.1.call-done = f32[144,1152]{1,0:T(8,128)} async-done(((f32[1152,1152]{1,0:T(8,128)}), f32[144,1152]{1,0:T(8,128)}) %reduce-scatter.33.cloned.1.call-update) | async-done | bytes 663568 | tf_op jit(solution)/shard_map/reduce_scatter | solution.py:322
  879.3 86.3 %reduce-scatter.29.cloned.1.call-done = f32[144,6,288]{2,0,1:T(8,128)} async-done(((f32[1152,6,288]{2,0,1:T(8,128)}), f32[144,6,288]{2,0,1:T(8,128)}) %reduce-scatter.29.cloned.1.call-update) | async-done | bytes 995344 | tf_op jit(solution)/shard_map/reduce_scatter | solution.py:319
  (286 shorter events, 39.8 us)
Async XLA Ops:
  7.2 10.7 %copy-start = (bf16[1152,1152]{1,0:T(8,128)(2,1)S(1)}, bf16[1152,1152]{1,0:T(8,128)(2,1)}, u32[]{:S(2)}) copy-start(bf16[1152,1152]{1,0:T(8,128)(2,1)} %param.37) | copy-start | bytes 7962628
  7.2 74.1 %all-gather.4.cloned.1.call-start = ((), (), s32[]{:S(2)}) async-start(), calls=%async_computation.13 | async-start | bytes 2949120 | tf_op jit(solution)/shard_map/all_gather | solution.py:121
  7.9 136.8 %reduce-scatter.13.cloned.1.call-start = ((), (), s32[]{:S(2)}) async-start(), calls=%async_computation.14 | async-start | bytes 2949120 | tf_op jit(solution)/shard_map/reduce_scatter | solution.py:151
  8.7 79.8 %copy-start.71 = (f32[72]{0:T(128)}, f32[72]{0:T(128)S(1)}, u32[]{:S(2)}) copy-start(f32[72]{0:T(128)S(1)} %convert_element_type.252) | copy-start | bytes 868
  9.3 79.4 %copy-start.73 = (f32[72]{0:T(128)}, f32[72]{0:T(128)S(1)}, u32[]{:S(2)}) copy-start(f32[72]{0:T(128)S(1)} %convert_element_type.255) | copy-start | bytes 868
  69.7 14.8 %copy-start.39 = (f32[4,6,1152]{2,0,1:T(4,128)}, f32[4,6,1152]{2,0,1:T(4,128)S(1)}, u32[]{:S(2)}) copy-start(f32[4,6,1152]{2,0,1:T(4,128)S(1)} %convert_element_type.248) | copy-start | bytes 331780
  70.0 14.5 %copy-start.55 = (f32[4,1152]{1,0:T(4,128)}, f32[4,1152]{1,0:T(4,128)S(1)}, u32[]{:S(2)}) copy-start(f32[4,1152]{1,0:T(4,128)S(1)} %get-tuple-element.150) | copy-start | bytes 55300
  70.0 14.5 %copy-start.57 = (f32[4,1152]{1,0:T(4,128)}, f32[4,1152]{1,0:T(4,128)S(1)}, u32[]{:S(2)}) copy-start(f32[4,1152]{1,0:T(4,128)S(1)} %get-tuple-element.151) | copy-start | bytes 55300
  81.3 2.4 copy-start.11
  83.5 1.6 copy-start.84
  83.7 4.1 copy-start.59
  84.5 3.4 copy-start.77
  87.9 4.9 copy-start.12
  88.1 1.6 copy-start.6
  88.4 1.6 copy-start.44
  88.4 1.6 copy-start.46
  88.4 1.6 copy-start.42
  90.4 1.6 copy-start.14
  90.4 1.6 copy-start.16
  90.4 1.6 copy-start.18
  92.1 2.0 copy-start.1
  94.9 3.2 copy-start.28
  98.2 46.6 %copy-start.3 = (bf16[1,256,1152]{2,1,0:T(8,128)(2,1)S(1)}, bf16[1,256,1152]{2,1,0:T(8,128)(2,1)}, u32[]{:S(2)}) copy-start(bf16[1,256,1152]{2,1,0:T(8,128)(2,1)} %param.20) | copy-start | bytes 1769476
  98.2 161.5 %all-gather.6.cloned.1.call-start = ((), (), s32[]{:S(2)}) async-start(), calls=%async_computation.16 | async-start | bytes 2949120 | tf_op jit(solution)/shard_map/all_gather | solution.py:184
  103.7 218.3 %reduce-scatter.17.cloned.1.call-start = ((), (), s32[]{:S(2)}) async-start(), calls=%async_computation.17 | async-start | bytes 2949120 | tf_op jit(solution)/shard_map/reduce_scatter | solution.py:196
  144.8 2.6 copy-start.32
  144.8 2.6 copy-start.34
  144.8 2.6 copy-start.48
  144.8 2.6 copy-start.53
  146.2 2.4 copy-start.54
  148.7 37.4 %collective-permute-start = (bf16[1,256,1152]{2,1,0:T(8,128)(2,1)}, bf16[1,256,1152]{2,1,0:T(8,128)(2,1)}, u32[]{:S(2)}, u32[]{:S(2)}) collective-permute-start(bf16[1,256,1152]{2,1,0:T(8,128)(2,1)} %add_convert_fusion), channel_id=1, source_target_pairs={{0,1},{1,0},{2,3},{3,2},{4,5},{5,4},{6,7},{7,6},{8,9},{9,8},{10,11... | collective-permute-start | bytes 1769480 | tf_op jit(solution)/shard_map/ppermute | solution.py:17
  188.9 60.4 %collective-permute-start.1 = (bf16[2,256,1152]{2,1,0:T(8,128)(2,1)}, bf16[2,256,1152]{2,1,0:T(8,128)(2,1)}, u32[]{:S(2)}, u32[]{:S(2)}) collective-permute-start(bf16[2,256,1152]{2,1,0:T(8,128)(2,1)} %maximum_select_fusion.1), channel_id=1, source_target_pairs={{0,2},{1,3},{2,0},{3,1},{4,6},{5,7},{6,4},{7,5},{8,10},{9,11},{10,... | collective-permute-start | bytes 3538952 | tf_op jit(solution)/shard_map/ppermute | solution.py:17
  259.7 10.0 %copy-start.83 = (bf16[1152,2,768]{2,1,0:T(2,128)(2,1)S(1)}, bf16[1152,2,768]{2,1,0:T(2,128)(2,1)}, u32[]{:S(2)}) copy-start(bf16[1152,2,768]{2,1,0:T(2,128)(2,1)} %param.30) | copy-start | bytes 10616836
  268.1 1.6 copy-start.89
  275.3 96.0 %reduce-scatter.15.cloned.1.call-start = ((), (), s32[]{:S(2)}) async-start(), calls=%async_computation.15 | async-start | bytes 2949120 | tf_op jit(solution)/shard_map/reduce_scatter | solution.py:172
  281.0 146.7 %all-gather.8.cloned.1.call-start = ((), (), s32[]{:S(2)}) async-start(), calls=%async_computation.18 | async-start | bytes 2949120 | tf_op jit(solution)/shard_map/all_gather | solution.py:209
  371.3 5.4 copy-start.33
  378.2 117.3 %reduce-scatter.19.cloned.1.call-start = ((), (), s32[]{:S(2)}) async-start(), calls=%async_computation.19 | async-start | bytes 2949120 | tf_op jit(solution)/shard_map/reduce_scatter | solution.py:248
  427.7 3.1 copy-start.2
  431.7 11.8 %copy-start.31 = (bf16[4,4,72,256]{3,2,1,0:T(8,128)(2,1)}, bf16[4,4,72,256]{3,2,1,0:T(8,128)(2,1)S(1)}, u32[]{:S(2)}) copy-start(bf16[4,4,72,256]{3,2,1,0:T(8,128)(2,1)S(1)} %convolution_convert_fusion.2) | copy-start | bytes 1769476
  440.5 3.0 copy-start.29
  443.0 1.8 copy-start.85
  448.9 115.0 %reduce-scatter.25.cloned.1.call-start = ((), (), s32[]{:S(2)}) async-start(), calls=%async_computation.22 | async-start | bytes 7962624 | tf_op jit(solution)/shard_map/reduce_scatter | solution.py:316
  459.6 174.0 %reduce-scatter.27.cloned.1.call-start = ((), (), s32[]{:S(2)}) async-start(), calls=%async_computation.23 | async-start | bytes 3981312 | tf_op jit(solution)/shard_map/reduce_scatter | solution.py:317
  465.7 193.9 %reduce-scatter.23.cloned.1.call-start = ((), (), s32[]{:S(2)}) async-start(), calls=%async_computation.21 | async-start | bytes 1990656 | tf_op jit(solution)/shard_map/reduce_scatter | solution.py:315
  470.3 250.0 %reduce-scatter.21.cloned.1.call-start = ((), (), s32[]{:S(2)}) async-start(), calls=%async_computation.20 | async-start | bytes 5971968 | tf_op jit(solution)/shard_map/reduce_scatter | solution.py:314
  479.2 16.4 %copy-start.49 = (f32[1152]{0:T(1024)S(1)}, f32[1152]{0:T(1024)}, u32[]{:S(2)}) copy-start(f32[1152]{0:T(1024)} %get-tuple-element.98) | copy-start | bytes 13828
  479.2 16.4 %copy-start.65 = (f32[256]{0:T(256)S(1)}, f32[256]{0:T(256)}, u32[]{:S(2)}) copy-start(f32[256]{0:T(256)} %broadcast_multiply_fusion.3) | copy-start | bytes 3076
  479.3 281.5 %reduce-scatter.31.cloned.1.call-start = ((), (), s32[]{:S(2)}) async-start(), calls=%async_computation.25 | async-start | bytes 1327104 | tf_op jit(solution)/shard_map/reduce_scatter | solution.py:320
  520.0 19.1 %copy-start.36 = (f32[4,1152]{1,0:T(4,128)S(1)}, f32[4,1152]{1,0:T(4,128)}, u32[]{:S(2)}) copy-start(f32[4,1152]{1,0:T(4,128)} %copy-done.35) | copy-start | bytes 55300
  520.0 19.1 %copy-start.38 = (f32[4,1152]{1,0:T(4,128)S(1)}, f32[4,1152]{1,0:T(4,128)}, u32[]{:S(2)}) copy-start(f32[4,1152]{1,0:T(4,128)} %copy-done.37) | copy-start | bytes 55300
  522.8 17.2 %copy-start.68 = (bf16[4,128]{1,0:T(4,128)(2,1)S(1)}, bf16[4,128]{1,0:T(4,128)(2,1)}, u32[]{:S(2)}) copy-start(bf16[4,128]{1,0:T(4,128)(2,1)} %copy-done.67) | copy-start | bytes 3076
  522.8 17.2 %copy-start.70 = (bf16[4,128]{1,0:T(4,128)(2,1)S(1)}, bf16[4,128]{1,0:T(4,128)(2,1)}, u32[]{:S(2)}) copy-start(bf16[4,128]{1,0:T(4,128)(2,1)} %copy-done.69) | copy-start | bytes 3076
  541.4 277.1 %reduce-scatter.35.cloned.1.call-start = ((), (), s32[]{:S(2)}) async-start(), calls=%async_computation.27 | async-start | bytes 5308416 | tf_op jit(solution)/shard_map/reduce_scatter | solution.py:318
  544.4 334.8 %reduce-scatter.33.cloned.1.call-start = ((), (), s32[]{:S(2)}) async-start(), calls=%async_computation.26 | async-start | bytes 5971968 | tf_op jit(solution)/shard_map/reduce_scatter | solution.py:322
  547.8 417.8 %reduce-scatter.29.cloned.1.call-start = ((), (), s32[]{:S(2)}) async-start(), calls=%async_computation.24 | async-start | bytes 11943936 | tf_op jit(solution)/shard_map/reduce_scatter | solution.py:319
  553.6 13.2 %copy-start.76 = (f32[256]{0:T(256)S(1)}, f32[256]{0:T(256)}, u32[]{:S(2)}) copy-start(f32[256]{0:T(256)} %get-tuple-element.92) | copy-start | bytes 3076
  553.6 13.2 %copy-start.75 = (f32[256]{0:T(256)S(1)}, f32[256]{0:T(256)}, u32[]{:S(2)}) copy-start(f32[256]{0:T(256)} %get-tuple-element.93) | copy-start | bytes 3076
  563.9 3.0 copy-start.10
  563.9 3.0 copy-start.13
  566.8 25.9 %copy-start.51 = (f32[1152]{0:T(1024)S(1)}, f32[1152]{0:T(1024)}, u32[]{:S(2)}) copy-start(f32[1152]{0:T(1024)} %get-tuple-element.114) | copy-start | bytes 13828
  566.8 25.9 %copy-start.52 = (f32[1152]{0:T(1024)S(1)}, f32[1152]{0:T(1024)}, u32[]{:S(2)}) copy-start(f32[1152]{0:T(1024)} %get-tuple-element.116) | copy-start | bytes 13828
  566.8 25.9 %copy-start.80 = (f32[72]{0:T(128)S(1)}, f32[72]{0:T(128)}, u32[]{:S(2)}) copy-start(f32[72]{0:T(128)} %get-tuple-element.85) | copy-start | bytes 868
  566.8 25.9 %copy-start.81 = (f32[72]{0:T(128)S(1)}, f32[72]{0:T(128)}, u32[]{:S(2)}) copy-start(f32[72]{0:T(128)} %get-tuple-element.87) | copy-start | bytes 868
  (43 other events, 44.4 us)
Sparse Core Ops, SparseCore 0:
  9.6 71.7 all-gather.3
  98.3 46.4 reduce-scatter.12
  146.9 69.3 all-gather.5
  275.4 46.5 reduce-scatter.16
  324.2 47.0 reduce-scatter.14
  378.4 49.3 all-gather.7
  449.1 46.4 reduce-scatter.18
  499.1 64.7 reduce-scatter.24
  568.0 48.4 reduce-scatter.26
  620.2 39.2 reduce-scatter.22
  663.5 56.7 reduce-scatter.20
  724.0 36.6 reduce-scatter.30
  764.7 53.7 reduce-scatter.34
  822.4 56.8 reduce-scatter.32
  883.2 82.3 reduce-scatter.28
